TPU v7x, 16 devices: a 4x2x1 block of a 4x4x8 slice. The times are simulated.
16 devices in a mesh: dp: 2 (over y, z), sp: 8 (over x, core).
Axes of the slice: x: 4, y: 2, z: 1, core: 2. Of those that a mesh axis runs over, the one named last changes fastest.
The devices are a block of a 4x4x8 slice.
Arguments:
- latent: bfloat16 [32, 64, 64, 4], P('dp', 'sp'), parts along dimension 0
- time_emb: bfloat16 [32, 1280], P('dp'), parts along dimension 0
- w_in: bfloat16 [3, 3, 4, 320], replicated
- b_in: bfloat16 [320], replicated
- gn1_scale: bfloat16 [2, 320], replicated
- gn1_shift: bfloat16 [2, 320], replicated
- conv1_w: bfloat16 [2, 3, 3, 320, 320], replicated
- conv1_b: bfloat16 [2, 320], replicated
- temb_w: bfloat16 [2, 1280, 320], replicated
- temb_b: bfloat16 [2, 320], replicated
- gn2_scale: bfloat16 [2, 320], replicated
- gn2_shift: bfloat16 [2, 320], replicated
- conv2_w: bfloat16 [2, 3, 3, 320, 320], replicated
- conv2_b: bfloat16 [2, 320], replicated
- down_w: bfloat16 [3, 3, 320, 320], replicated
- down_b: bfloat16 [320], replicated
Outputs:
- output 1: bfloat16 [32, 64, 64, 320], P('dp', 'sp'), parts along dimension 0
- output 2: bfloat16 [32, 64, 64, 320], P('dp', 'sp'), parts along dimension 0
- output 3: bfloat16 [32, 64, 64, 320], P('dp', 'sp'), parts along dimension 0
- output 4: bfloat16 [32, 32, 32, 320], P('dp', 'sp'), parts along dimension 0
There are 2 independent parts. A program takes and returns all parts, laid end to end along the dimension named above; an argument that names none is the same for every part.
All inputs are finite; a program needn't handle non-finite values.
Results may differ from a plain program's by a relative error of at most 0.0134522.
Values are sent between devices in bfloat16 or wider.
A program may use at most 768 MiB of HBM per device.

v0:
```python
import jax
import jax.numpy as jnp
from jax import lax
from jax.sharding import PartitionSpec as P

GN_GROUPS = 32
GN_EPS = 1e-5
DIM_NUMS = ("NHWC", "HWIO", "NHWC")


def conv_valid_rows(inputs, kernel, bias_c, stride):
    out_f32 = lax.conv_general_dilated(inputs, kernel, (stride, stride), ((0, 0), (1, 1)), dimension_numbers=DIM_NUMS, preferred_element_type=jnp.float32)
    return (out_f32 + bias_c.astype(jnp.float32)).astype(jnp.bfloat16)


def group_sums(values):
    batch_n, rows_n, cols_n, chan_n = values.shape
    grouped = values.reshape(batch_n, rows_n * cols_n, GN_GROUPS, chan_n // GN_GROUPS)
    return jnp.stack([grouped.sum(axis=(1, 3)), jnp.square(grouped).sum(axis=(1, 3))], axis=-1)


def norm_silu(values, sums_all, elem_count, gain_c, shift_c):
    group_ch = values.shape[-1] // GN_GROUPS
    grp_mean = sums_all[..., 0] / elem_count
    grp_var = sums_all[..., 1] / elem_count - grp_mean * grp_mean
    inv_std = lax.rsqrt(grp_var + GN_EPS)
    scale_bc = jnp.repeat(inv_std, group_ch, axis=1) * gain_c.astype(jnp.float32)
    offset_bc = shift_c.astype(jnp.float32) - jnp.repeat(grp_mean, group_ch, axis=1) * scale_bc
    return jax.nn.silu(values * scale_bc[:, None, None, :] + offset_bc[:, None, None, :]).astype(jnp.bfloat16)


def solution(mesh):
    sp_size = mesh.shape["sp"]
    to_next = [(device, device + 1) for device in range(sp_size - 1)]
    to_prev = [(device + 1, device) for device in range(sp_size - 1)]

    def row_from_above(band_block):
        return lax.ppermute(band_block[:, -1:], "sp", to_next)

    def row_from_below(band_block):
        return lax.ppermute(band_block[:, :1], "sp", to_prev)

    def conv_band(band_block, kernel, bias_c):
        padded = jnp.concatenate([row_from_above(band_block), band_block, row_from_below(band_block)], axis=1)
        return conv_valid_rows(padded, kernel, bias_c, 1)

    def band_program(latent, time_emb, w_in, b_in, gn1_scale, gn1_shift, conv1_w, conv1_b, temb_w, temb_b, gn2_scale, gn2_shift, conv2_w, conv2_b, down_w, down_b):
        elem_count = latent.shape[1] * sp_size * latent.shape[2] * (w_in.shape[-1] // GN_GROUPS)
        emb_act = jax.nn.silu(time_emb.astype(jnp.float32)).astype(jnp.bfloat16)
        hidden = conv_band(latent, w_in, b_in)
        outputs = [hidden]
        for layer_idx in range(conv1_w.shape[0]):
            hidden_f32 = hidden.astype(jnp.float32)
            sums_all = lax.psum(group_sums(hidden_f32), "sp")
            normed = norm_silu(hidden_f32, sums_all, elem_count, gn1_scale[layer_idx], gn1_shift[layer_idx])
            branch = conv_band(normed, conv1_w[layer_idx], conv1_b[layer_idx])
            emb_proj = jnp.dot(emb_act, temb_w[layer_idx], preferred_element_type=jnp.float32) + temb_b[layer_idx].astype(jnp.float32)
            mixed_in = branch.astype(jnp.float32) + emb_proj[:, None, None, :]
            sums_all = lax.psum(group_sums(mixed_in), "sp")
            normed = norm_silu(mixed_in, sums_all, elem_count, gn2_scale[layer_idx], gn2_shift[layer_idx])
            branch = conv_band(normed, conv2_w[layer_idx], conv2_b[layer_idx])
            hidden = (hidden_f32 + branch.astype(jnp.float32)).astype(jnp.bfloat16)
            outputs.append(hidden)
        padded = jnp.concatenate([row_from_above(hidden), hidden], axis=1)
        outputs.append(conv_valid_rows(padded, down_w, down_b, 2))
        return tuple(outputs)

    band_spec = P("dp", "sp", None, None)
    return jax.shard_map(band_program, mesh=mesh, in_specs=(band_spec, P("dp", None)) + (P(),) * 14, out_specs=(band_spec,) * 4, check_vma=False)
```

profile of v0, /device:TPU:113, one launch (start us, length us, event | category | flops | bytes accessed | tf_op | source)
XLA Modules:
  0.0 348.4 jit_solution(15429304872349361472)
XLA Ops:
  0.6 1.5 copy.42
  2.2 4.6 %collective-permute-start = (bf16[16,1,64,4]{0,3,2,1:T(4,128)(2,1)S(1)}, bf16[16,1,64,4]{0,3,2,1:T(4,128)(2,1)S(1)}, u32[]{:S(2)}, u32[]{:S(2)}) collective-permute-start(bf16[16,1,64,4]{0,3,2,1:T(4,128)(2,1)S(1)} %get-tuple-element.58), channel_id=1, source_target_pairs={{0,1},{1,2},{2,3},{3,4},{4,5},{5,6},{6,7},{8,9},{9,10},{10,11},{11... | collective-permute-start | bytes 24584 | tf_op jit(solution)/shard_map/ppermute | solution.py:38
  6.8 2.0 collective-permute-start.1
  8.8 0.8 convert_reduce_fusion.7
  9.6 0.7 convert_element_type.126
  10.3 2.2 collective-permute-done.1
  12.5 6.7 %convert_reduce_fusion.1 = (f32[16,320]{1,0:T(8,128)S(1)}, f32[16,320]{1,0:T(8,128)S(1)}, bf16[16,8,64,320]{3,0,2,1:T(8,128)(2,1)}) fusion(f32[320]{0:T(512)S(1)} %convert_element_type.126, bf16[3,3,4,320]{3,2,1,0:T(4,128)(2,1)} %param.18, bf16[16,1,64,4]{0,3,2,1:T(4,128)(2,1)S(1)} %collective-permute-done.1, bf16[16,8,64,4]{0,3,2,1:T(4,128)(2,1)S(1)} %copy.42, ...), kind=kOutput, calls=%fused_computation.7 | convolution fusion | flops 202741760 | bytes 5390080 | tf_op jit(solution)/shard_map/conv_general_dilated | solution.py:12
  19.4 0.3 reduce_sum.99
  20.0 20.4 %psum.28 = f32[16,32,2]{1,0,2:T(8,128)S(1)} all-reduce(f32[16,32,2]{1,0,2:T(8,128)S(1)} %pad_maximum_fusion), channel_id=1, replica_groups=mesh['dp'=2,'sp'=8] {'sp'}, use_global_device_ids=true, to_apply=%region_4.5 | all-reduce | flops 1024 | bytes 8192 | tf_op jit(solution)/shard_map/psum | solution.py:54
  41.1 5.8 %fusion.7 = bf16[16,8,64,320]{3,0,2,1:T(8,128)(2,1)S(1)} fusion(bf16[16,8,64,320]{3,0,2,1:T(8,128)(2,1)} %get-tuple-element.60, f32[16,320]{1,0:T(8,128)S(1)} %get-tuple-element.48, f32[16,320]{1,0:T(8,128)S(1)} %get-tuple-element.49), kind=kLoop, calls=%fused_computation.15 | loop fusion | flops 20971520 | bytes 10526720 | tf_op jit(solution)/shard_map/convert_element_type | solution.py:29
  47.1 3.6 %collective-permute-start.2 = (bf16[16,1,64,320]{3,0,2,1:T(8,128)(2,1)S(1)}, bf16[16,1,64,320]{3,0,2,1:T(8,128)(2,1)S(1)}, u32[]{:S(2)}, u32[]{:S(2)}) collective-permute-start(bf16[16,1,64,320]{3,0,2,1:T(8,128)(2,1)S(1)} %get-tuple-element.56), channel_id=1, source_target_pairs={{0,1},{1,2},{2,3},{3,4},{4,5},{5,6},{6,7},{8,9},{9,10},{10,11},{11... | collective-permute-start | bytes 1966088 | tf_op jit(solution)/shard_map/ppermute | solution.py:38
  50.8 3.7 %collective-permute-start.3 = (bf16[16,1,64,320]{3,0,2,1:T(8,128)(2,1)S(1)}, bf16[16,1,64,320]{3,0,2,1:T(8,128)(2,1)S(1)}, u32[]{:S(2)}, u32[]{:S(2)}) collective-permute-start(bf16[16,1,64,320]{3,0,2,1:T(8,128)(2,1)S(1)} %get-tuple-element.57), channel_id=1, source_target_pairs={{1,0},{2,1},{3,2},{4,3},{5,4},{6,5},{7,6},{9,8},{10,9},{11,10},{12... | collective-permute-start | bytes 1966088 | tf_op jit(solution)/shard_map/ppermute | solution.py:41
  54.6 0.3 convolution_add_fusion.1
  54.9 4.8 %collective-permute-done.2 = bf16[16,1,64,320]{3,0,2,1:T(8,128)(2,1)S(1)} collective-permute-done((bf16[16,1,64,320]{3,0,2,1:T(8,128)(2,1)S(1)}, bf16[16,1,64,320]{3,0,2,1:T(8,128)(2,1)S(1)}, u32[]{:S(2)}, u32[]{:S(2)}) %collective-permute-start.2) | collective-permute-done | bytes 655392 | tf_op jit(solution)/shard_map/ppermute | solution.py:38
  59.6 4.4 %collective-permute-done.3 = bf16[16,1,64,320]{3,0,2,1:T(8,128)(2,1)S(1)} collective-permute-done((bf16[16,1,64,320]{3,0,2,1:T(8,128)(2,1)S(1)}, bf16[16,1,64,320]{3,0,2,1:T(8,128)(2,1)S(1)}, u32[]{:S(2)}, u32[]{:S(2)}) %collective-permute-start.3) | collective-permute-done | bytes 655392 | tf_op jit(solution)/shard_map/ppermute | solution.py:41
  64.1 30.6 %fusion.19 = (f32[16,320]{1,0:T(8,128)S(1)}, f32[16,320]{1,0:T(8,128)S(1)}, bf16[16,8,64,320]{3,0,2,1:T(8,128)(2,1)}) fusion(f32[16,320]{1,0:T(8,128)S(1)} %convolution_add_fusion.1, f32[320]{0:T(512)S(1)} %get-tuple-element.39, bf16[2,3,3,320,320]{4,3,2,1,0:T(8,128)(2,1)} %param.22, bf16[16,1,64,320]{3,0,2,1:T(8,128)(2,1)S(1)} %collective-permute-done.3, ...), kind=kOutput, calls=%fused_computation.36 | convolution fusion | flops 14980208640 | bytes 14071040 | tf_op jit(solution)/shard_map/conv_general_dilated | solution.py:12
  95.1 0.3 reduce_sum.111
  95.6 20.4 %psum.29 = f32[16,32,2]{1,0,2:T(8,128)S(1)} all-reduce(f32[16,32,2]{1,0,2:T(8,128)S(1)} %pad_maximum_fusion.1), channel_id=1, replica_groups=mesh['dp'=2,'sp'=8] {'sp'}, use_global_device_ids=true, to_apply=%region_9.10 | all-reduce | flops 1024 | bytes 8192 | tf_op jit(solution)/shard_map/psum | solution.py:59
  116.6 5.9 %multiply_convert_fusion.1 = bf16[16,8,64,320]{3,0,2,1:T(8,128)(2,1)S(1)} fusion(bf16[16,8,64,320]{3,0,2,1:T(8,128)(2,1)} %get-tuple-element.61, f32[16,320]{1,0:T(8,128)S(1)} %get-tuple-element.46, f32[16,320]{1,0:T(8,128)S(1)} %get-tuple-element.47, f32[16,320]{1,0:T(8,128)S(1)} %convolution_add_fusion.1), kind=kLoop, calls=%fused_computation.33 | loop fusion | flops 23592960 | bytes 10547200 | tf_op jit(solution)/shard_map/convert_element_type | solution.py:29
  122.8 3.6 %collective-permute-start.4 = (bf16[16,1,64,320]{3,0,2,1:T(8,128)(2,1)S(1)}, bf16[16,1,64,320]{3,0,2,1:T(8,128)(2,1)S(1)}, u32[]{:S(2)}, u32[]{:S(2)}) collective-permute-start(bf16[16,1,64,320]{3,0,2,1:T(8,128)(2,1)S(1)} %get-tuple-element.54), channel_id=1, source_target_pairs={{0,1},{1,2},{2,3},{3,4},{4,5},{5,6},{6,7},{8,9},{9,10},{10,11},{11... | collective-permute-start | bytes 1966088 | tf_op jit(solution)/shard_map/ppermute | solution.py:38
  126.4 3.4 collective-permute-start.5
  129.8 5.5 %collective-permute-done.4 = bf16[16,1,64,320]{3,0,2,1:T(8,128)(2,1)S(1)} collective-permute-done((bf16[16,1,64,320]{3,0,2,1:T(8,128)(2,1)S(1)}, bf16[16,1,64,320]{3,0,2,1:T(8,128)(2,1)S(1)}, u32[]{:S(2)}, u32[]{:S(2)}) %collective-permute-start.4) | collective-permute-done | bytes 655392 | tf_op jit(solution)/shard_map/ppermute | solution.py:38
  135.3 4.4 %collective-permute-done.5 = bf16[16,1,64,320]{3,0,2,1:T(8,128)(2,1)S(1)} collective-permute-done((bf16[16,1,64,320]{3,0,2,1:T(8,128)(2,1)S(1)}, bf16[16,1,64,320]{3,0,2,1:T(8,128)(2,1)S(1)}, u32[]{:S(2)}, u32[]{:S(2)}) %collective-permute-start.5) | collective-permute-done | bytes 655392 | tf_op jit(solution)/shard_map/ppermute | solution.py:41
  139.7 31.9 %convert_reduce_fusion = (f32[16,320]{1,0:T(8,128)S(1)}, f32[16,320]{1,0:T(8,128)S(1)}, bf16[16,8,64,320]{3,0,2,1:T(8,128)(2,1)}) fusion(f32[320]{0:T(512)S(1)} %get-tuple-element.41, bf16[2,3,3,320,320]{4,3,2,1,0:T(8,128)(2,1)} %param.28, bf16[16,1,64,320]{3,0,2,1:T(8,128)(2,1)S(1)} %collective-permute-done.5, ...), kind=kOutput, calls=%fused_computation.3 | convolution fusion | flops 14988072960 | bytes 20342016 | tf_op jit(solution)/shard_map/conv_general_dilated | solution.py:12
  172.1 0.3 reduce_sum.144
  172.5 20.4 %psum.30 = f32[16,32,2]{1,0,2:T(8,128)S(1)} all-reduce(f32[16,32,2]{1,0,2:T(8,128)S(1)} %pad_maximum_fusion.2), channel_id=1, replica_groups=mesh['dp'=2,'sp'=8] {'sp'}, use_global_device_ids=true, to_apply=%region_14.15 | all-reduce | flops 1024 | bytes 8192 | tf_op jit(solution)/shard_map/psum | solution.py:54
  193.6 5.8 %fusion.16 = bf16[16,8,64,320]{3,0,2,1:T(8,128)(2,1)S(1)} fusion(bf16[16,8,64,320]{3,0,2,1:T(8,128)(2,1)} %get-tuple-element.62, f32[16,320]{1,0:T(8,128)S(1)} %get-tuple-element.44, f32[16,320]{1,0:T(8,128)S(1)} %get-tuple-element.45), kind=kLoop, calls=%fused_computation.24 | loop fusion | flops 20971520 | bytes 10526720 | tf_op jit(solution)/shard_map/convert_element_type | solution.py:29
  199.5 3.6 %collective-permute-start.6 = (bf16[16,1,64,320]{3,0,2,1:T(8,128)(2,1)S(1)}, bf16[16,1,64,320]{3,0,2,1:T(8,128)(2,1)S(1)}, u32[]{:S(2)}, u32[]{:S(2)}) collective-permute-start(bf16[16,1,64,320]{3,0,2,1:T(8,128)(2,1)S(1)} %get-tuple-element.52), channel_id=1, source_target_pairs={{0,1},{1,2},{2,3},{3,4},{4,5},{5,6},{6,7},{8,9},{9,10},{10,11},{11... | collective-permute-start | bytes 1966088 | tf_op jit(solution)/shard_map/ppermute | solution.py:38
  203.2 3.4 collective-permute-start.7
  206.6 0.3 convolution_add_fusion
  206.9 5.1 %collective-permute-done.6 = bf16[16,1,64,320]{3,0,2,1:T(8,128)(2,1)S(1)} collective-permute-done((bf16[16,1,64,320]{3,0,2,1:T(8,128)(2,1)S(1)}, bf16[16,1,64,320]{3,0,2,1:T(8,128)(2,1)S(1)}, u32[]{:S(2)}, u32[]{:S(2)}) %collective-permute-start.6) | collective-permute-done | bytes 655392 | tf_op jit(solution)/shard_map/ppermute | solution.py:38
  212.1 4.4 %collective-permute-done.7 = bf16[16,1,64,320]{3,0,2,1:T(8,128)(2,1)S(1)} collective-permute-done((bf16[16,1,64,320]{3,0,2,1:T(8,128)(2,1)S(1)}, bf16[16,1,64,320]{3,0,2,1:T(8,128)(2,1)S(1)}, u32[]{:S(2)}, u32[]{:S(2)}) %collective-permute-start.7) | collective-permute-done | bytes 655392 | tf_op jit(solution)/shard_map/ppermute | solution.py:41
  216.5 30.6 %fusion.18 = (f32[16,320]{1,0:T(8,128)S(1)}, f32[16,320]{1,0:T(8,128)S(1)}, bf16[16,8,64,320]{3,0,2,1:T(8,128)(2,1)}) fusion(f32[16,320]{1,0:T(8,128)S(1)} %convolution_add_fusion, f32[320]{0:T(512)S(1)} %get-tuple-element.38, bf16[2,3,3,320,320]{4,3,2,1,0:T(8,128)(2,1)} %param.22, bf16[16,1,64,320]{3,0,2,1:T(8,128)(2,1)S(1)} %collective-permute-done.7, ...), kind=kOutput, calls=%fused_computation.30 | convolution fusion | flops 14980208640 | bytes 14071040 | tf_op jit(solution)/shard_map/conv_general_dilated | solution.py:12
  247.6 0.3 reduce_sum.150
  248.0 20.4 %psum.31 = f32[16,32,2]{1,0,2:T(8,128)S(1)} all-reduce(f32[16,32,2]{1,0,2:T(8,128)S(1)} %pad_maximum_fusion.3), channel_id=1, replica_groups=mesh['dp'=2,'sp'=8] {'sp'}, use_global_device_ids=true, to_apply=%region_19.20 | all-reduce | flops 1024 | bytes 8192 | tf_op jit(solution)/shard_map/psum | solution.py:59
  269.1 6.7 %multiply_convert_fusion = bf16[16,8,64,320]{3,0,2,1:T(8,128)(2,1)S(1)} fusion(bf16[16,8,64,320]{3,0,2,1:T(8,128)(2,1)} %get-tuple-element.63, f32[16,320]{1,0:T(8,128)S(1)} %get-tuple-element.42, f32[16,320]{1,0:T(8,128)S(1)} %get-tuple-element.43, f32[16,320]{1,0:T(8,128)S(1)} %convolution_add_fusion), kind=kLoop, calls=%fused_computation.27 | loop fusion | flops 23592960 | bytes 10547200 | tf_op jit(solution)/shard_map/convert_element_type | solution.py:29
  275.9 3.6 %collective-permute-start.8 = (bf16[16,1,64,320]{3,0,2,1:T(8,128)(2,1)S(1)}, bf16[16,1,64,320]{3,0,2,1:T(8,128)(2,1)S(1)}, u32[]{:S(2)}, u32[]{:S(2)}) collective-permute-start(bf16[16,1,64,320]{3,0,2,1:T(8,128)(2,1)S(1)} %get-tuple-element.50), channel_id=1, source_target_pairs={{0,1},{1,2},{2,3},{3,4},{4,5},{5,6},{6,7},{8,9},{9,10},{10,11},{11... | collective-permute-start | bytes 1966088 | tf_op jit(solution)/shard_map/ppermute | solution.py:38
  279.6 3.6 %collective-permute-start.9 = (bf16[16,1,64,320]{3,0,2,1:T(8,128)(2,1)S(1)}, bf16[16,1,64,320]{3,0,2,1:T(8,128)(2,1)S(1)}, u32[]{:S(2)}, u32[]{:S(2)}) collective-permute-start(bf16[16,1,64,320]{3,0,2,1:T(8,128)(2,1)S(1)} %get-tuple-element.51), channel_id=1, source_target_pairs={{1,0},{2,1},{3,2},{4,3},{5,4},{6,5},{7,6},{9,8},{10,9},{11,10},{12... | collective-permute-start | bytes 1966088 | tf_op jit(solution)/shard_map/ppermute | solution.py:41
  283.2 5.3 %collective-permute-done.8 = bf16[16,1,64,320]{3,0,2,1:T(8,128)(2,1)S(1)} collective-permute-done((bf16[16,1,64,320]{3,0,2,1:T(8,128)(2,1)S(1)}, bf16[16,1,64,320]{3,0,2,1:T(8,128)(2,1)S(1)}, u32[]{:S(2)}, u32[]{:S(2)}) %collective-permute-start.8) | collective-permute-done | bytes 655392 | tf_op jit(solution)/shard_map/ppermute | solution.py:38
  288.5 4.4 %collective-permute-done.9 = bf16[16,1,64,320]{3,0,2,1:T(8,128)(2,1)S(1)} collective-permute-done((bf16[16,1,64,320]{3,0,2,1:T(8,128)(2,1)S(1)}, bf16[16,1,64,320]{3,0,2,1:T(8,128)(2,1)S(1)}, u32[]{:S(2)}, u32[]{:S(2)}) %collective-permute-start.9) | collective-permute-done | bytes 655392 | tf_op jit(solution)/shard_map/ppermute | solution.py:41
  292.9 29.3 %fusion.17 = bf16[16,8,64,320]{3,0,2,1:T(8,128)(2,1)S(1)} fusion(bf16[16,8,64,320]{3,0,2,1:T(8,128)(2,1)} %get-tuple-element.62, f32[320]{0:T(512)S(1)} %get-tuple-element.40, bf16[16,1,64,320]{3,0,2,1:T(8,128)(2,1)S(1)} %collective-permute-done.9, bf16[16,8,64,320]{3,0,2,1:T(8,128)(2,1)S(1)} %multiply_convert_fusion, ...), kind=kOutput, calls=%fused_computation.25 | convolution fusion | flops 14977597440 | bytes 20301056 | tf_op jit(solution)/shard_map/conv_general_dilated | solution.py:12
  322.2 2.7 copy-done.1
  324.9 2.1 collective-permute-start.10
  327.1 4.3 %copy.45 = bf16[16,8,64,320]{3,2,1,0:T(8,128)(2,1)} copy(bf16[16,8,64,320]{3,0,2,1:T(8,128)(2,1)S(1)} %bitcast.83) | data formatting | bytes 10485760
  331.4 4.3 %copy.46 = bf16[16,8,64,320]{3,2,1,0:T(8,128)(2,1)} copy(bf16[16,8,64,320]{3,0,2,1:T(8,128)(2,1)S(1)} %bitcast.85) | data formatting | bytes 10485760
  335.7 4.3 %copy.47 = bf16[16,8,64,320]{3,2,1,0:T(8,128)(2,1)} copy(bf16[16,8,64,320]{3,0,2,1:T(8,128)(2,1)S(1)} %copy-done.2) | data formatting | bytes 10485760
  340.0 6.7 %add_convert_fusion.5 = bf16[16,4,32,320]{3,0,2,1:T(8,128)(2,1)S(1)} fusion(bf16[3,3,320,320]{3,2,1,0:T(8,128)(2,1)S(1)} %copy-done, bf16[16,8,64,320]{3,0,2,1:T(8,128)(2,1)S(1)} %copy-done.2, bf16[16,1,64,320]{3,0,2,1:T(8,128)(2,1)S(1)} %collective-permute-done.10, f32[320]{0:T(512)S(1)} %convert_element_type.154), kind=kOutput, calls=%fused_computation.67 | convolution fusion | flops 3748659200 | bytes 9053440 | tf_op jit(solution)/shard_map/conv_general_dilated | solution.py:12
  346.7 1.5 copy.48
  (90 shorter events, 5.6 us)
Async XLA Ops:
  0.6 339.4 %copy-start = (bf16[3,3,320,320]{3,2,1,0:T(8,128)(2,1)S(1)}, bf16[3,3,320,320]{3,2,1,0:T(8,128)(2,1)}, u32[]{:S(2)}) copy-start(bf16[3,3,320,320]{3,2,1,0:T(8,128)(2,1)} %param.30) | copy-start | bytes 5529604
  2.2 8.1 %collective-permute-start = (bf16[16,1,64,4]{0,3,2,1:T(4,128)(2,1)S(1)}, bf16[16,1,64,4]{0,3,2,1:T(4,128)(2,1)S(1)}, u32[]{:S(2)}, u32[]{:S(2)}) collective-permute-start(bf16[16,1,64,4]{0,3,2,1:T(4,128)(2,1)S(1)} %get-tuple-element.58), channel_id=1, source_target_pairs={{0,1},{1,2},{2,3},{3,4},{4,5},{5,6},{6,7},{8,9},{9,10},{10,11},{11... | collective-permute-start | bytes 24584 | tf_op jit(solution)/shard_map/ppermute | solution.py:38
  6.8 5.6 %collective-permute-start.1 = (bf16[16,1,64,4]{0,3,2,1:T(4,128)(2,1)S(1)}, bf16[16,1,64,4]{0,3,2,1:T(4,128)(2,1)S(1)}, u32[]{:S(2)}, u32[]{:S(2)}) collective-permute-start(bf16[16,1,64,4]{0,3,2,1:T(4,128)(2,1)S(1)} %get-tuple-element.59), channel_id=1, source_target_pairs={{1,0},{2,1},{3,2},{4,3},{5,4},{6,5},{7,6},{9,8},{10,9},{11,10},{12... | collective-permute-start | bytes 24584 | tf_op jit(solution)/shard_map/ppermute | solution.py:41
  41.1 13.4 %copy-start.3 = (bf16[2,320]{1,0:T(2,128)(2,1)S(1)}, bf16[2,320]{1,0:T(2,128)(2,1)}, u32[]{:S(2)}) copy-start(bf16[2,320]{1,0:T(2,128)(2,1)} %param.25) | copy-start | bytes 3844
  41.1 13.4 %copy-start.4 = (bf16[2,320]{1,0:T(2,128)(2,1)S(1)}, bf16[2,320]{1,0:T(2,128)(2,1)}, u32[]{:S(2)}) copy-start(bf16[2,320]{1,0:T(2,128)(2,1)} %param.23) | copy-start | bytes 3844
  41.1 13.4 %copy-start.5 = (bf16[2,320]{1,0:T(2,128)(2,1)S(1)}, bf16[2,320]{1,0:T(2,128)(2,1)}, u32[]{:S(2)}) copy-start(bf16[2,320]{1,0:T(2,128)(2,1)} %param.27) | copy-start | bytes 3844
  41.1 13.4 %copy-start.6 = (bf16[2,320]{1,0:T(2,128)(2,1)S(1)}, bf16[2,320]{1,0:T(2,128)(2,1)}, u32[]{:S(2)}) copy-start(bf16[2,320]{1,0:T(2,128)(2,1)} %param.26) | copy-start | bytes 3844
  41.1 13.4 %copy-start.9 = (bf16[2,1280,320]{1,2,0:T(8,128)(2,1)S(1)}, bf16[2,1280,320]{1,2,0:T(8,128)(2,1)}, u32[]{:S(2)}) copy-start(bf16[2,1280,320]{1,2,0:T(8,128)(2,1)} %param.24) | copy-start | bytes 4915204
  41.1 13.4 %copy-start.11 = (bf16[16,1280]{1,0:T(8,128)(2,1)S(1)}, bf16[16,1280]{1,0:T(8,128)(2,1)}, u32[]{:S(2)}) copy-start(bf16[16,1280]{1,0:T(8,128)(2,1)} %param.17) | copy-start | bytes 122884
  47.1 12.5 %collective-permute-start.2 = (bf16[16,1,64,320]{3,0,2,1:T(8,128)(2,1)S(1)}, bf16[16,1,64,320]{3,0,2,1:T(8,128)(2,1)S(1)}, u32[]{:S(2)}, u32[]{:S(2)}) collective-permute-start(bf16[16,1,64,320]{3,0,2,1:T(8,128)(2,1)S(1)} %get-tuple-element.56), channel_id=1, source_target_pairs={{0,1},{1,2},{2,3},{3,4},{4,5},{5,6},{6,7},{8,9},{9,10},{10,11},{11... | collective-permute-start | bytes 1966088 | tf_op jit(solution)/shard_map/ppermute | solution.py:38
  50.8 13.3 %collective-permute-start.3 = (bf16[16,1,64,320]{3,0,2,1:T(8,128)(2,1)S(1)}, bf16[16,1,64,320]{3,0,2,1:T(8,128)(2,1)S(1)}, u32[]{:S(2)}, u32[]{:S(2)}) collective-permute-start(bf16[16,1,64,320]{3,0,2,1:T(8,128)(2,1)S(1)} %get-tuple-element.57), channel_id=1, source_target_pairs={{1,0},{2,1},{3,2},{4,3},{5,4},{6,5},{7,6},{9,8},{10,9},{11,10},{12... | collective-permute-start | bytes 1966088 | tf_op jit(solution)/shard_map/ppermute | solution.py:41
  116.6 13.2 %copy-start.7 = (bf16[2,320]{1,0:T(2,128)(2,1)S(1)}, bf16[2,320]{1,0:T(2,128)(2,1)}, u32[]{:S(2)}) copy-start(bf16[2,320]{1,0:T(2,128)(2,1)} %param.29) | copy-start | bytes 3844
  122.8 12.5 %collective-permute-start.4 = (bf16[16,1,64,320]{3,0,2,1:T(8,128)(2,1)S(1)}, bf16[16,1,64,320]{3,0,2,1:T(8,128)(2,1)S(1)}, u32[]{:S(2)}, u32[]{:S(2)}) collective-permute-start(bf16[16,1,64,320]{3,0,2,1:T(8,128)(2,1)S(1)} %get-tuple-element.54), channel_id=1, source_target_pairs={{0,1},{1,2},{2,3},{3,4},{4,5},{5,6},{6,7},{8,9},{9,10},{10,11},{11... | collective-permute-start | bytes 1966088 | tf_op jit(solution)/shard_map/ppermute | solution.py:38
  126.4 13.3 %collective-permute-start.5 = (bf16[16,1,64,320]{3,0,2,1:T(8,128)(2,1)S(1)}, bf16[16,1,64,320]{3,0,2,1:T(8,128)(2,1)S(1)}, u32[]{:S(2)}, u32[]{:S(2)}) collective-permute-start(bf16[16,1,64,320]{3,0,2,1:T(8,128)(2,1)S(1)} %get-tuple-element.55), channel_id=1, source_target_pairs={{1,0},{2,1},{3,2},{4,3},{5,4},{6,5},{7,6},{9,8},{10,9},{11,10},{12... | collective-permute-start | bytes 1966088 | tf_op jit(solution)/shard_map/ppermute | solution.py:41
  193.5 13.0 %copy-start.10 = (bf16[2,1280,320]{1,2,0:T(8,128)(2,1)S(1)}, bf16[2,1280,320]{1,2,0:T(8,128)(2,1)}, u32[]{:S(2)}) copy-start(bf16[2,1280,320]{1,2,0:T(8,128)(2,1)} %param.24) | copy-start | bytes 4915204
  199.5 12.5 %collective-permute-start.6 = (bf16[16,1,64,320]{3,0,2,1:T(8,128)(2,1)S(1)}, bf16[16,1,64,320]{3,0,2,1:T(8,128)(2,1)S(1)}, u32[]{:S(2)}, u32[]{:S(2)}) collective-permute-start(bf16[16,1,64,320]{3,0,2,1:T(8,128)(2,1)S(1)} %get-tuple-element.52), channel_id=1, source_target_pairs={{0,1},{1,2},{2,3},{3,4},{4,5},{5,6},{6,7},{8,9},{9,10},{10,11},{11... | collective-permute-start | bytes 1966088 | tf_op jit(solution)/shard_map/ppermute | solution.py:38
  203.2 13.3 %collective-permute-start.7 = (bf16[16,1,64,320]{3,0,2,1:T(8,128)(2,1)S(1)}, bf16[16,1,64,320]{3,0,2,1:T(8,128)(2,1)S(1)}, u32[]{:S(2)}, u32[]{:S(2)}) collective-permute-start(bf16[16,1,64,320]{3,0,2,1:T(8,128)(2,1)S(1)} %get-tuple-element.53), channel_id=1, source_target_pairs={{1,0},{2,1},{3,2},{4,3},{5,4},{6,5},{7,6},{9,8},{10,9},{11,10},{12... | collective-permute-start | bytes 1966088 | tf_op jit(solution)/shard_map/ppermute | solution.py:41
  269.1 58.0 %slice-start = ((s8[6291456]{0:T(1024)(128)(4,1)}), s8[4194304]{0:T(1024)(128)(4,1)S(1)}, s32[]{:S(2)}) async-start(s8[6291456]{0:T(1024)(128)(4,1)} %bitcast.82), calls=%async_computation | async-start | bytes 8388608
  269.1 62.3 %slice-start.2 = ((s8[6291456]{0:T(1024)(128)(4,1)}), s8[4194304]{0:T(1024)(128)(4,1)S(1)}, s32[]{:S(2)}) async-start(s8[6291456]{0:T(1024)(128)(4,1)} %bitcast.84), calls=%async_computation.2 | async-start | bytes 8388608
  275.9 12.5 %collective-permute-start.8 = (bf16[16,1,64,320]{3,0,2,1:T(8,128)(2,1)S(1)}, bf16[16,1,64,320]{3,0,2,1:T(8,128)(2,1)S(1)}, u32[]{:S(2)}, u32[]{:S(2)}) collective-permute-start(bf16[16,1,64,320]{3,0,2,1:T(8,128)(2,1)S(1)} %get-tuple-element.50), channel_id=1, source_target_pairs={{0,1},{1,2},{2,3},{3,4},{4,5},{5,6},{6,7},{8,9},{9,10},{10,11},{11... | collective-permute-start | bytes 1966088 | tf_op jit(solution)/shard_map/ppermute | solution.py:38
  279.6 13.3 %collective-permute-start.9 = (bf16[16,1,64,320]{3,0,2,1:T(8,128)(2,1)S(1)}, bf16[16,1,64,320]{3,0,2,1:T(8,128)(2,1)S(1)}, u32[]{:S(2)}, u32[]{:S(2)}) collective-permute-start(bf16[16,1,64,320]{3,0,2,1:T(8,128)(2,1)S(1)} %get-tuple-element.51), channel_id=1, source_target_pairs={{1,0},{2,1},{3,2},{4,3},{5,4},{6,5},{7,6},{9,8},{10,9},{11,10},{12... | collective-permute-start | bytes 1966088 | tf_op jit(solution)/shard_map/ppermute | solution.py:41
  292.9 34.2 %copy-start.8 = (bf16[320]{0:T(512)(128)(2,1)S(1)}, bf16[320]{0:T(512)(128)(2,1)}, u32[]{:S(2)}) copy-start(bf16[320]{0:T(512)(128)(2,1)} %param.31) | copy-start | bytes 1924
  292.9 34.2 %slice-start.1 = ((s8[6291456]{0:T(1024)(128)(4,1)}), s8[2097152]{0:T(1024)(128)(4,1)S(1)}, s32[]{:S(2)}) async-start(s8[6291456]{0:T(1024)(128)(4,1)} %bitcast.82), calls=%async_computation.1 | async-start | bytes 4194304
  292.9 38.5 %slice-start.3 = ((s8[6291456]{0:T(1024)(128)(4,1)}), s8[2097152]{0:T(1024)(128)(4,1)S(1)}, s32[]{:S(2)}) async-start(s8[6291456]{0:T(1024)(128)(4,1)} %bitcast.84), calls=%async_computation.3 | async-start | bytes 4194304
  322.2 2.7 copy-start.1
  324.9 15.1 %collective-permute-start.10 = (bf16[16,1,64,320]{3,0,2,1:T(8,128)(2,1)S(1)}, bf16[16,1,64,320]{3,0,2,1:T(8,128)(2,1)S(1)}, u32[]{:S(2)}, u32[]{:S(2)}) collective-permute-start(bf16[16,1,64,320]{3,0,2,1:T(8,128)(2,1)S(1)} %slice.174), channel_id=1, source_target_pairs={{0,1},{1,2},{2,3},{3,4},{4,5},{5,6},{6,7},{8,9},{9,10},{10,11},{11... | collective-permute-start | bytes 1966088 | tf_op jit(solution)/shard_map/ppermute | solution.py:38
  331.4 4.3 %copy-start.2 = (bf16[16,8,64,320]{3,0,2,1:T(8,128)(2,1)S(1)}, bf16[16,8,64,320]{3,0,2,1:T(8,128)(2,1)}, u32[]{:S(2)}) copy-start(bf16[16,8,64,320]{3,0,2,1:T(8,128)(2,1)} %copy-done.1) | copy-start | bytes 15728644
where the time goes:
time: 353 us; the launch traced here: 348 us
  matrix products  136 us (39%)
  blocking collectives  81.8 us (23%)
  waiting for transfers between devices  40.6 us (12%)
  starting transfers between devices  37.3 us (11%)
  other arithmetic  27 us (8%)
  local copies, waits for them, and re-layouts  23.8 us (7%)
    conv_general_dilated x6, matrix products, conv_valid_rows(): lax.conv_general_dilated(inputs, kernel, (stride, stride), ((0, 0), (1, 1...  136 us
    psum x2, blocking collectives, band_program(): sums_all = lax.psum(group_sums(hidden_f32), 'sp')  40.9 us
    psum x2, blocking collectives, band_program(): sums_all = lax.psum(group_sums(mixed_in), 'sp')  40.9 us
    convert_element_type x4, other arithmetic, norm_silu(): jax.nn.silu(values * scale_bc[:, None, None, :] + offset_bc[:, None, None...  24.2 us
    ppermute x6, starting transfers between devices, row_from_above(): return lax.ppermute(band_block[:, -1:], 'sp', to_next)  21.3 us
    ppermute x6, waiting for transfers between devices, row_from_above(): return lax.ppermute(band_block[:, -1:], 'sp', to_next)  20.7 us
    ppermute x5, waiting for transfers between devices, row_from_below(): return lax.ppermute(band_block[:, :1], 'sp', to_prev)  20 us
    unnamed x37, local copies, waits for them, and re-layouts  18.6 us
  transfers between devices with their start and end apart: 11, of which 9 were waited for; matrix products, arithmetic and copies ran while one was open for 4% of the time, Pallas kernels for 0%

commit v1 on v0

v1 whole, which is shorter than its diff:
```python
import functools

import jax
import jax.numpy as jnp
from jax import lax
from jax.experimental import pallas as pl
from jax.experimental.pallas import tpu as pltpu
from jax.sharding import PartitionSpec as P

GN_GROUPS = 32
GN_EPS = 1e-5
MESH = pl.DeviceIdType.MESH
F32 = jnp.float32
BF16 = jnp.bfloat16
LANES = 384
MAIN = 256


def lane_ids():
    return lax.broadcasted_iota(jnp.int32, (8, LANES), 1)


def all_sublane_sum(x):
    x = x + pltpu.roll(x, 4, 0)
    x = x + pltpu.roll(x, 2, 0)
    return x + pltpu.roll(x, 1, 0)


def roll_left(x, k):
    return pltpu.roll(x, LANES - k, 1)


def group_window(x):
    x2 = x + roll_left(x, 1)
    x4 = x2 + roll_left(x2, 2)
    x8 = x4 + roll_left(x4, 4)
    return x8 + roll_left(x2, 8)


def group_spread(x):
    x2 = x + pltpu.roll(x, 1, 1)
    x4 = x2 + pltpu.roll(x2, 2, 1)
    x8 = x4 + pltpu.roll(x4, 4, 1)
    return x8 + pltpu.roll(x2, 8, 1)


def kernel(n_sp, count, patches, time_emb, w_in, b_in, gn1_scale, gn1_shift, conv1_b, temb_b, gn2_scale, gn2_shift, conv2_b, down_b,
           conv1_w, conv2_w, temb_w, down_w,
           out0, out1, out2, outd,
           act0, act1, halo, xs_a, xs_b, raw, wmain, wrem, temb_buf, etab, prow, stat_in, stat_out, acc_s, dstage, dbuf,
           halo_recv, stat_recv, halo_send, stat_send, w_sem, t_sem, o_sem):
    n_batch, n_rows, n_cols, chan = act0.shape
    tail = chan - MAIN
    me = lax.axis_index("sp")
    above = lax.rem(me + n_sp - 1, n_sp)
    below = lax.rem(me + 1, n_sp)
    half = n_rows * n_cols
    layers = conv1_w.shape[0]
    acts = (act0, act1)
    xs = (xs_a, xs_b)

    barrier = pltpu.get_barrier_semaphore()
    for d in range(1, n_sp):
        pl.semaphore_signal(barrier, inc=1, device_id={"sp": lax.rem(me + d, n_sp)}, device_id_type=MESH)
    pl.semaphore_wait(barrier, n_sp - 1)

    def w_copy(q):
        src = down_w if q == 2 * layers else (conv1_w, conv2_w)[q % 2].at[q // 2]
        return pltpu.make_async_copy(src, raw.at[q % 2], w_sem.at[q % 2])

    temb_copy = pltpu.make_async_copy(temb_w, temb_buf, t_sem)
    temb_copy.start()
    w_copy(0).start()

    for ref, q0 in ((gn1_scale, 0), (gn2_scale, 1)):
        for l in range(layers):
            prow[3 * (2 * l + q0), :, 0:chan] = jnp.broadcast_to(ref[l:l + 1, :].astype(F32), (8, chan))
    for ref, q0 in ((gn1_shift, 0), (gn2_shift, 1)):
        for l in range(layers):
            prow[3 * (2 * l + q0) + 1, :, 0:chan] = jnp.broadcast_to(ref[l:l + 1, :].astype(F32), (8, chan))
    for ref, q0 in ((conv1_b, 0), (conv2_b, 1)):
        for l in range(layers):
            prow[3 * (2 * l + q0) + 2, :, 0:chan] = jnp.broadcast_to(ref[l:l + 1, :].astype(F32), (8, chan))
    prow[6 * layers, :, 0:chan] = jnp.broadcast_to(b_in[...].astype(F32), (8, chan))
    prow[6 * layers + 1, :, 0:chan] = jnp.broadcast_to(down_b[...].astype(F32), (8, chan))
    for k in range(6 * layers + 2):
        prow[k, :, chan:LANES] = jnp.zeros((8, LANES - chan), F32)
    acc_s[...] = jnp.zeros(acc_s.shape, F32)
    for x in xs:
        x[:, :, 3 * MAIN + 3 * tail:] = jnp.zeros(x.shape[:2] + (x.shape[2] - 3 * MAIN - 3 * tail,), BF16)

    def send_halo(q, s):
        par = q % 2
        up = pltpu.make_async_remote_copy(acts[par].at[s, 0], halo.at[q, s, 1], halo_send.at[s, 0], halo_recv.at[q, s, 1], device_id={"sp": above}, device_id_type=MESH)
        down = pltpu.make_async_remote_copy(acts[par].at[s, n_rows - 1], halo.at[q, s, 0], halo_send.at[s, 1], halo_recv.at[q, s, 0], device_id={"sp": below}, device_id_type=MESH)
        return up, down

    def send_stats(q, s):
        return [pltpu.make_async_remote_copy(stat_out.at[s], stat_in.at[q, s, me], stat_send.at[s, d - 1], stat_recv.at[q, s], device_id={"sp": lax.rem(me + d, n_sp)}, device_id_type=MESH) for d in range(1, n_sp)]

    def wait_sends(s):
        for cp in send_halo(0, s):
            cp.wait_send()
        for cp in send_stats(0, s):
            cp.wait_send()

    def wait_stats(q, s):
        part = stat_in.at[q, s, pl.ds(0, n_sp - 1)]
        pltpu.make_async_copy(part, part, stat_recv.at[q, s]).wait()

    def wait_halo(q, s):
        for k in range(2):
            pltpu.make_async_copy(halo.at[q, s, k], halo.at[q, s, k], halo_recv.at[q, s, k]).wait()

    def put_stats(q, s, k, sums):
        group_ch = chan // GN_GROUPS
        (sm, qm), (st, qt) = sums
        acc_s[2 * k, :, 0:MAIN] = sm
        acc_s[2 * k, :, MAIN:chan] = st
        acc_s[2 * k + 1, :, 0:MAIN] = qm
        acc_s[2 * k + 1, :, MAIN:chan] = qt
        s8 = all_sublane_sum(acc_s[2 * k])
        q8 = all_sublane_sum(acc_s[2 * k + 1])
        sub = lax.broadcasted_iota(jnp.int32, (8, LANES), 0)
        win = group_window(jnp.where(sub < 4, s8, q8))
        lane = lane_ids()
        win = jnp.where((lax.rem(lane, group_ch) == 0) & (lane < chan), win, 0.0)
        row = win[0:1] + pltpu.roll(win, group_ch // 2, 1)[4:5]
        stat_out[s] = row
        stat_in[q, s, me] = row

    def affine(q, s):
        group_ch = chan // GN_GROUPS
        row = jnp.sum(stat_in[q, s], axis=0)
        tot = jnp.broadcast_to(row, (8, LANES))
        lane = lane_ids()
        sub = lax.broadcasted_iota(jnp.int32, (8, LANES), 0)
        rem = lax.rem(lane, group_ch)
        z = jnp.where(sub < 4, jnp.where(rem == 0, tot, 0.0), roll_left(jnp.where(rem == group_ch // 2, tot, 0.0), group_ch // 2))
        z = group_spread(z) * (1.0 / count)
        mean = jnp.broadcast_to(z[0:1], (8, LANES))
        sq = jnp.broadcast_to(z[4:5], (8, LANES))
        inv = lax.rsqrt(sq - mean * mean + GN_EPS)
        scale = inv * prow[3 * q]
        off = prow[3 * q + 1] - mean * scale
        if q % 2:
            off = off + etab[q // 2, s] * scale
        return 0.5 * scale, 0.5 * off

    def act_fn(x, scale, off):
        r, c = x.shape
        z = (x.reshape(r // 8, 8, c) * scale[None] + off[None]).reshape(r, c)
        return z + z * jnp.tanh(z)

    def norm_stage(q, s, dst):
        scale, off = affine(q, s)
        col_m = lax.broadcasted_iota(jnp.int32, (n_cols, MAIN), 0)
        col_t = lax.broadcasted_iota(jnp.int32, (n_cols, tail), 0)

        def shifts(y, col):
            left = jnp.where(col == 0, 0.0, pltpu.roll(y, 1, 0))
            right = jnp.where(col == n_cols - 1, 0.0, pltpu.roll(y, n_cols - 1, 0))
            return left, right

        for r in range(n_rows + 2):
            if r == 0:
                row = halo.at[q, s, 0]
            elif r == n_rows + 1:
                row = halo.at[q, s, 1]
            else:
                row = acts[q % 2].at[s, r - 1]
            ym = act_fn(row[:, 0:MAIN].astype(F32), scale[:, 0:MAIN], off[:, 0:MAIN])
            yt = act_fn(row[:, MAIN:chan].astype(F32), scale[:, MAIN:chan], off[:, MAIN:chan])
            if r == 0:
                keep = jnp.where(me > 0, 1.0, 0.0)
                ym, yt = ym * keep, yt * keep
            if r == n_rows + 1:
                keep = jnp.where(me < n_sp - 1, 1.0, 0.0)
                ym, yt = ym * keep, yt * keep
            lm, rm = shifts(ym, col_m)
            lt, rt = shifts(yt, col_t)
            dst[r, :, 0:MAIN] = lm.astype(BF16)
            dst[r, :, MAIN:2 * MAIN] = ym.astype(BF16)
            dst[r, :, 2 * MAIN:3 * MAIN] = rm.astype(BF16)
            dst[r, :, 3 * MAIN:3 * MAIN + 2 * tail] = jnp.concatenate([lt, yt], axis=1).astype(BF16)
            dst[r, :, 3 * MAIN + 2 * tail:3 * MAIN + 3 * tail] = rt.astype(BF16)

    def col_sums(x):
        v = x.reshape(x.shape[0] // 8, 8, x.shape[1])
        return v.sum(axis=0), (v * v).sum(axis=0)

    def add_pair(a, b):
        return (b if a is None else (a[0] + b[0], a[1] + b[1]))

    def tile_row(x, rows):
        return jnp.broadcast_to(x[None], (rows // 8, 8, x.shape[1])).reshape(rows, x.shape[1])

    def finish(q, s, k, main, rest):
        bias = prow[6 * layers if q < 0 else 3 * q + 2]
        dst = acts[(q + 1) % 2]
        nxt = q + 1
        sums_m = sums_t = None
        for r in range(n_rows):
            rows = slice(r * n_cols, (r + 1) * n_cols)
            tm = (main(r) + tile_row(bias[:, 0:MAIN], n_cols)).astype(BF16)
            tt = (rest(r) + tile_row(bias[:, MAIN:chan], n_cols)).astype(BF16)
            if q >= 0 and q % 2:
                tm = (dst[s, r, :, 0:MAIN].astype(F32) + tm.astype(F32)).astype(BF16)
                tt = (dst[s, r, :, MAIN:chan].astype(F32) + tt.astype(F32)).astype(BF16)
            dst[s, r, :, 0:MAIN] = tm
            dst[s, r, :, MAIN:chan] = tt
            if nxt < 2 * layers:
                vm, vt = tm.astype(F32), tt.astype(F32)
                if nxt % 2:
                    e = etab[nxt // 2, s]
                    vm = vm + tile_row(e[:, 0:MAIN], n_cols)
                    vt = vt + tile_row(e[:, MAIN:chan], n_cols)
                sums_m = add_pair(sums_m, col_sums(vm))
                sums_t = add_pair(sums_t, col_sums(vt))
        if nxt < 2 * layers:
            put_stats(nxt, s, k, (sums_m, sums_t))

    def conv_stage(q, s, k, src):
        lhs = jnp.concatenate([src[dy:dy + n_rows].reshape(half, 4 * MAIN) for dy in range(3)], axis=1)
        main = jnp.dot(lhs, wmain[...], preferred_element_type=F32)
        rest = jnp.dot(src[...].reshape(half + 2 * n_cols, 4 * MAIN), wrem[...], preferred_element_type=F32)

        def main_row(r):
            return main[r * n_cols:(r + 1) * n_cols]

        def rest_row(r):
            p0 = rest[r * n_cols:(r + 1) * n_cols, 0:tail]
            p1 = rest[(r + 1) * n_cols:(r + 2) * n_cols, tail:2 * tail]
            p2 = rest[(r + 2) * n_cols:(r + 3) * n_cols, 2 * tail:3 * tail]
            return p0 + p1 + p2

        finish(q, s, k, main_row, rest_row)

    def start_sends(q, s):
        for cp in send_halo(q, s):
            cp.start()
        if q < 2 * layers:
            for cp in send_stats(q, s):
                cp.start()

    def load_weights(q):
        w_copy(q).wait()
        if q < 2 * layers:
            w_copy(q + 1).start()
        par = q % 2
        for dy in range(3):
            for dx in range(3):
                wmain[dy * 1024 + dx * MAIN:dy * 1024 + (dx + 1) * MAIN, :] = raw[par, dy, dx, 0:MAIN, 0:MAIN]
                wmain[dy * 1024 + 3 * MAIN + dx * tail:dy * 1024 + 3 * MAIN + (dx + 1) * tail, :] = raw[par, dy, dx, MAIN:chan, 0:MAIN]
            wmain[dy * 1024 + 3 * MAIN + 3 * tail:(dy + 1) * 1024, :] = jnp.zeros((MAIN - 3 * tail, MAIN), BF16)
        for dx in range(3):
            for lo, n, at in ((0, MAIN, dx * MAIN), (MAIN, tail, 3 * MAIN + dx * tail)):
                w01 = jnp.concatenate([raw[par, dy, dx, lo:lo + n, MAIN:chan].astype(F32) for dy in range(2)], axis=1)
                wrem[at:at + n, 0:2 * tail] = w01.astype(BF16)
                w2 = jnp.concatenate([raw[par, 2, dx, lo:lo + n, MAIN:chan].astype(F32), jnp.zeros((n, tail), F32)], axis=1)
                wrem[at:at + n, 2 * tail:] = w2.astype(BF16)
        wrem[3 * MAIN + 3 * tail:, :] = jnp.zeros((MAIN - 3 * tail, MAIN), BF16)

    temb_copy.wait()
    emb = time_emb[...].astype(F32)
    emb = (emb * jax.nn.sigmoid(emb)).astype(BF16)
    for l in range(layers):
        e = jnp.dot(emb, temb_buf[l], preferred_element_type=F32) + temb_b[l:l + 1, :].astype(F32)
        for s in range(n_batch):
            etab[l, s, :, 0:chan] = jnp.broadcast_to(e[s:s + 1], (8, chan))
            etab[l, s, :, chan:LANES] = jnp.zeros((8, LANES - chan), F32)

    @pl.loop(0, n_batch // 2)
    def _(j):
        for k in range(2):
            s = 2 * j + k
            out = jnp.dot(patches[s], w_in[...], preferred_element_type=F32)
            finish(-1, s, k, lambda r: out[r * n_cols:(r + 1) * n_cols, 0:MAIN], lambda r: out[r * n_cols:(r + 1) * n_cols, MAIN:chan])
        for k in range(2):
            start_sends(0, 2 * j + k)

    outs = (out0, out1, out2)

    def out_copy(i):
        return pltpu.make_async_copy(act0, outs[i], o_sem)

    out_copy(0).start()
    wait_stats(0, 0)
    wait_halo(0, 0)
    norm_stage(0, 0, xs_a)

    def pair(q, j, last):
        s0 = 2 * j
        targets = [(q, s0 + 1), (q + 1, 0) if last else (q, s0 + 2)]
        for tq, ts in targets:
            if tq < 2 * layers:
                wait_stats(tq, ts)
                wait_halo(tq, ts)
        for k in range(2):
            wait_sends(s0 + k)
        for k in range(2):
            tq, ts = targets[k]
            if tq < 2 * layers:
                norm_stage(tq, ts, xs[1 - k])
            conv_stage(q, s0 + k, k, xs[k])
        for k in range(2):
            start_sends(q + 1, s0 + k)

    for q in range(2 * layers):
        load_weights(q)
        if q % 2:
            out_copy(q // 2).wait()

        @pl.loop(0, n_batch // 2 - 1)
        def _(j):
            pair(q, j, False)

        pair(q, n_batch // 2 - 1, True)
        if q % 2:
            out_copy(q // 2 + 1).start()

    w_copy(2 * layers).wait()
    par = (2 * layers) % 2
    bias = prow[6 * layers + 1]
    half_cols = n_cols // 2
    out_rows = n_rows // 2

    @pl.loop(0, n_batch // 2)
    def _(j):
        for k in range(2):
            for cp in send_halo(0, 2 * j + k):
                cp.wait_send()
            pltpu.make_async_copy(halo.at[2 * layers, 2 * j + k, 1], halo.at[2 * layers, 2 * j + k, 1], halo_recv.at[2 * layers, 2 * j + k, 1]).wait()
            pltpu.make_async_copy(halo.at[2 * layers, 2 * j + k, 0], halo.at[2 * layers, 2 * j + k, 0], halo_recv.at[2 * layers, 2 * j + k, 0]).wait()
        for k in range(2):
            s = 2 * j + k
            for r in range(n_rows + 1):
                row = halo.at[2 * layers, s, 0] if r == 0 else acts[0].at[s, r - 1]
                x = row[...].astype(F32)
                if r == 0:
                    x = x * jnp.where(me > 0, 1.0, 0.0)
                for c in range(3):
                    width = min(128, chan - 128 * c)
                    dstage[k, r, c, :, 0:width] = x[:, 128 * c:128 * c + width]
            for r in range(n_rows + 1):
                evens, odds = [], []
                for c in range(3):
                    width = min(128, chan - 128 * c)
                    evens.append(dstage[k, r, c, pl.ds(0, half_cols, 2), :][:, 0:width])
                    odds.append(dstage[k, r, c, pl.ds(1, half_cols, 2), :][:, 0:width])
                col = lax.broadcasted_iota(jnp.int32, (half_cols, 1), 0)
                lefts = [jnp.where(col == 0, 0.0, pltpu.roll(o, 1, 0)) for o in odds]
                dst = xs[k]
                hc = slice(0, half_cols)
                for at, parts in ((0, lefts), (MAIN, evens), (2 * MAIN, odds)):
                    dst[r, hc, at:at + 128] = parts[0].astype(BF16)
                    dst[r, hc, at + 128:at + 256] = parts[1].astype(BF16)
                dst[r, hc, 3 * MAIN:3 * MAIN + 2 * tail] = jnp.concatenate([lefts[2], evens[2]], axis=1).astype(BF16)
                dst[r, hc, 3 * MAIN + 2 * tail:3 * MAIN + 3 * tail] = odds[2].astype(BF16)
        parts = []
        for k in range(2):
            rows = []
            for ro in range(out_rows):
                rows.append(jnp.concatenate([xs[k][2 * ro + dy, 0:half_cols, :] for dy in range(3)], axis=1))
            parts.append(jnp.concatenate(rows, axis=0))
        lhs = jnp.concatenate(parts, axis=0)
        acc = None
        for dy in range(3):
            for dx in range(3):
                a = jnp.dot(lhs[:, dy * 1024 + dx * MAIN:dy * 1024 + (dx + 1) * MAIN], raw[par, dy, dx, 0:MAIN, :], preferred_element_type=F32)
                acc = a if acc is None else acc + a
            wt = jnp.concatenate([raw[par, dy, dx, MAIN:chan, :] for dx in range(3)] + [jnp.zeros((MAIN - 3 * tail, chan), BF16)], axis=0)
            acc = acc + jnp.dot(lhs[:, dy * 1024 + 3 * MAIN:(dy + 1) * 1024], wt, preferred_element_type=F32)
        acc = acc.reshape(2 * out_rows * half_cols // 8, 8, chan) + bias[None, :, 0:chan]
        dbuf[pl.ds(2 * j, 2)] = acc.astype(BF16).reshape(2, out_rows, half_cols, chan)

    d_copy = pltpu.make_async_copy(dbuf, outd, t_sem)
    d_copy.start()
    out_copy(layers).wait()
    d_copy.wait()


def solution(mesh):
    n_sp = mesh.shape["sp"]
    to_next = [(i, (i + 1) % n_sp) for i in range(n_sp)]
    to_prev = [((i + 1) % n_sp, i) for i in range(n_sp)]

    def band_program(latent, time_emb, w_in, b_in, gn1_scale, gn1_shift, conv1_w, conv1_b, temb_w, temb_b, gn2_scale, gn2_shift, conv2_w, conv2_b, down_w, down_b):
        n_batch, n_rows, n_cols, lat = latent.shape
        chan = w_in.shape[-1]
        layers = conv1_w.shape[0]
        me = lax.axis_index("sp")
        top = lax.ppermute(latent[:, -1:], "sp", to_next[:-1])
        bot = lax.ppermute(latent[:, :1], "sp", to_prev[:-1])
        band = jnp.concatenate([top, latent, bot], axis=1)
        band = jnp.pad(band, ((0, 0), (0, 0), (1, 1), (0, 0)))
        patches = jnp.concatenate([band[:, dy:dy + n_rows, dx:dx + n_cols] for dy in range(3) for dx in range(3)], axis=-1)
        patches = patches.reshape(n_batch, n_rows * n_cols, 9 * lat)
        count = float(n_rows * n_sp * n_cols * (chan // GN_GROUPS))
        vmem = pl.BlockSpec(memory_space=pltpu.VMEM)
        anym = pl.BlockSpec(memory_space=pl.ANY)
        band_shape = jax.ShapeDtypeStruct((n_batch, n_rows, n_cols, chan), BF16)
        down_shape = jax.ShapeDtypeStruct((n_batch, n_rows // 2, n_cols // 2, chan), BF16)
        nq = 2 * layers
        return pl.pallas_call(
            functools.partial(kernel, n_sp, count),
            out_shape=(band_shape,) * 3 + (down_shape,),
            in_specs=[vmem] * 12 + [anym] * 4,
            out_specs=(anym,) * 4,
            scratch_shapes=[
                pltpu.VMEM((n_batch, n_rows, n_cols, chan), BF16),
                pltpu.VMEM((n_batch, n_rows, n_cols, chan), BF16),
                pltpu.VMEM((nq + 1, n_batch, 2, n_cols, chan), BF16),
                pltpu.VMEM((n_rows + 2, n_cols, 4 * MAIN), BF16),
                pltpu.VMEM((n_rows + 2, n_cols, 4 * MAIN), BF16),
                pltpu.VMEM((2, 3, 3, chan, chan), BF16),
                pltpu.VMEM((12 * MAIN, MAIN), BF16),
                pltpu.VMEM((4 * MAIN, MAIN), BF16),
                pltpu.VMEM(temb_w.shape, BF16),
                pltpu.VMEM((layers, n_batch, 8, LANES), F32),
                pltpu.VMEM((6 * layers + 2, 8, LANES), F32),
                pltpu.VMEM((nq, n_batch, n_sp, 1, LANES), F32),
                pltpu.VMEM((n_batch, 1, LANES), F32),
                pltpu.VMEM((4, 8, LANES), F32),
                pltpu.VMEM((2, n_rows + 1, 3, n_cols, 128), F32),
                pltpu.VMEM((n_batch, n_rows // 2, n_cols // 2, chan), BF16),
                pltpu.SemaphoreType.DMA((nq + 1, n_batch, 2)),
                pltpu.SemaphoreType.DMA((nq, n_batch)),
                pltpu.SemaphoreType.DMA((n_batch, 2)),
                pltpu.SemaphoreType.DMA((n_batch, n_sp - 1)),
                pltpu.SemaphoreType.DMA((2,)),
                pltpu.SemaphoreType.DMA,
                pltpu.SemaphoreType.DMA,
            ],
            compiler_params=pltpu.CompilerParams(collective_id=0, has_side_effects=True, vmem_limit_bytes=60 * 1024 * 1024),
        )(patches, time_emb, w_in.reshape(9 * lat, chan), b_in.reshape(1, chan), gn1_scale, gn1_shift, conv1_b, temb_b, gn2_scale, gn2_shift, conv2_b, down_b.reshape(1, chan),
          conv1_w, conv2_w, temb_w, down_w)

    band_spec = P("dp", "sp", None, None)
    return jax.shard_map(band_program, mesh=mesh, in_specs=(band_spec, P("dp", None)) + (P(),) * 14, out_specs=(band_spec,) * 4, check_vma=False)
```

time: 353 us -> 185 us (0.52); the launches traced: 348 us -> 185 us
  Pallas kernels: 0 us -> 148 us
  matrix products: 136 us -> 0 us
  blocking collectives: 81.8 us -> 0 us
  waiting for transfers between devices: 40.6 us -> 0.01 us
  starting transfers between devices: 37.3 us -> 6.56 us
  other arithmetic: 27 us -> 2.63 us
    pallas_call x0 -> x1, Pallas kernels: none -> 148 us  [band_program(): pl.pallas_call(functools.partial(kernel, n_sp, count), out_shape=(band_sh...]
    conv_general_dilated x6 -> x0, matrix products: 136 us -> none  [conv_valid_rows(): lax.conv_general_dilated(inputs, kernel, (stride, stride), ((0, 0), (1, 1...]
    psum x4 -> x0, blocking collectives: 81.8 us -> none  [the longest x2 40.9 us: band_program(): sums_all = lax.psum(group_sums(hidden_f32), 'sp')]
    ppermute x11 -> x2, waiting for transfers between devices: 40.6 us -> 0.01 us  [the longest x1 0.01 us: band_program(): top = lax.ppermute(latent[:, -1:], 'sp', to_next[:-1])]
    ppermute x11 -> x2, starting transfers between devices: 37.3 us -> 6.56 us  [the longest x1 4.6 us: band_program(): top = lax.ppermute(latent[:, -1:], 'sp', to_next[:-1])]
    convert_element_type x8 -> x0, other arithmetic: 24.9 us -> none  [the longest x4 24.2 us: norm_silu(): jax.nn.silu(values * scale_bc[:, None, None, :] + offset_bc[:, None, None...]
    concatenate x0 -> x2, local copies, waits for them, and re-layouts: none -> 4.34 us  [band_program(): jnp.concatenate([band[:, dy:dy + n_rows, dx:dx + n_cols] for dy in range(...]
    unnamed x37 -> x15, local copies, waits for them, and re-layouts: 18.6 us -> 17.9 us
  transfers between devices with their start and end apart: 11 -> 2, of which waited for: 9 -> 0; matrix products, arithmetic and copies ran while one was open for 4% -> 4% of each run, Pallas kernels for 0% -> 0%
where the time goes in v1:
time: 185 us
  Pallas kernels  148 us (80%)
  local copies, waits for them, and re-layouts  26.9 us (15%)
  starting transfers between devices  6.56 us (4%)
  other arithmetic  2.63 us (1%)
    pallas_call x1, Pallas kernels, band_program(): pl.pallas_call(functools.partial(kernel, n_sp, count), out_shape=(band_sh...  148 us
    unnamed x15, local copies, waits for them, and re-layouts  17.9 us
    ppermute x1, starting transfers between devices, band_program(): top = lax.ppermute(latent[:, -1:], 'sp', to_next[:-1])  4.6 us
    concatenate x2, local copies, waits for them, and re-layouts, band_program(): jnp.concatenate([band[:, dy:dy + n_rows, dx:dx + n_cols] for dy in range(...  4.34 us
  transfers between devices with their start and end apart: 2, of which 0 were waited for; matrix products, arithmetic and copies ran while one was open for 4% of the time, Pallas kernels for 0%

profile of v1, /device:TPU:113, one launch (start us, length us, event | category | flops | bytes accessed | tf_op | source)
XLA Modules:
  0.0 185.0 jit_solution(14542251919755005542)
XLA Ops:
  0.6 0.0 copy-start.2
  0.6 0.8 fusion.2
  1.4 4.6 %collective-permute-start = (bf16[16,1,64,4]{2,3,1,0:T(4,128)(2,1)S(1)}, bf16[16,1,64,4]{2,3,1,0:T(4,128)(2,1)S(1)}, u32[]{:S(2)}, u32[]{:S(2)}) collective-permute-start(bf16[16,1,64,4]{2,3,1,0:T(4,128)(2,1)S(1)} %get-tuple-element.12), channel_id=1, source_target_pairs={{0,1},{1,2},{2,3},{3,4},{4,5},{5,6},{6,7},{8,9},{9,10},{10,11},{11... | collective-permute-start | bytes 24584 | tf_op jit(solution)/shard_map/ppermute | solution.py:393
  6.1 2.0 %collective-permute-start.1 = (bf16[16,1,64,4]{2,3,1,0:T(4,128)(2,1)S(1)}, bf16[16,1,64,4]{2,3,1,0:T(4,128)(2,1)S(1)}, u32[]{:S(2)}, u32[]{:S(2)}) collective-permute-start(bf16[16,1,64,4]{2,3,1,0:T(4,128)(2,1)S(1)} %get-tuple-element.13), channel_id=1, source_target_pairs={{1,0},{2,1},{3,2},{4,3},{5,4},{6,5},{7,6},{9,8},{10,9},{11,10},{12... | collective-permute-start | bytes 24584 | tf_op jit(solution)/shard_map/ppermute | solution.py:394
  8.0 1.2 reshape.22.b_in
  9.3 1.2 reshape.23.down_b
  10.5 1.4 reshape.21.w_in
  11.9 3.6 %copy.21.temb_w = bf16[2,1280,320]{2,1,0:T(8,128)(2,1)} copy(bf16[2,1280,320]{1,2,0:T(8,128)(2,1)} %param.24) | data formatting | bytes 3276800 | tf_op args[8]
  15.5 0.0 collective-permute-done
  15.5 0.0 collective-permute-done.1
  15.5 1.1 select_maximum_fusion
  16.6 1.5 pad_maximum_fusion
  18.1 0.0 copy-done.2
  18.2 1.2 concatenate.15
  19.4 3.1 %copy.20 = bf16[16,8,64,36]{3,2,1,0:T(8,128)(2,1)} copy(bf16[16,8,64,36]{2,3,1,0:T(8,128)(2,1)S(1)} %concatenate.15) | data formatting | bytes 1179648 | tf_op jit(solution)/shard_map/concatenate | solution.py:397
  22.5 148.2 %shard_map.183 = (bf16[16,8,64,320]{3,2,1,0:T(8,128)(2,1)}, bf16[16,8,64,320]{3,2,1,0:T(8,128)(2,1)}, bf16[16,8,64,320]{3,2,1,0:T(8,128)(2,1)}, bf16[16,4,32,320]{3,2,1,0:T(8,128)(2,1)}) custom-call(bf16[16,512,36]{2,1,0:T(8,128)(2,1)} %bitcast.1, bf16[16,1280]{1,0:T(8,128)(2,1)} %time_emb.1, bf16[36,320]{1,0:T(8,128)(2,1)} %reshape.21.w_in, ...), custom_call_target="tpu_custom_call" | custom-call | tf_op jit(solution)/shard_map/pallas_call | solution.py:405
  170.7 0.0 copy-start
  170.7 0.0 slice-start
  170.7 7.1 %copy.26 = bf16[16,8,64,320]{3,2,1,0:T(8,128)(2,1)} copy(bf16[16,8,64,320]{3,2,1,0:T(8,128)(2,1)} %get-tuple-element.24) | data formatting | bytes 10485760
  177.8 0.0 copy-done
  177.8 0.0 slice-start.1
  177.8 2.8 %copy.27 = bf16[16,8,64,320]{3,2,1,0:T(8,128)(2,1)} copy(bf16[16,8,64,320]{3,2,1,0:T(8,128)(2,1)S(1)} %copy-done) | data formatting | bytes 10485760
  180.6 0.0 slice-done
  180.6 0.5 slice-done.1
  181.1 0.0 copy-start.1
  181.1 2.7 %copy.28 = bf16[16,8,64,320]{3,2,1,0:T(8,128)(2,1)} copy(bf16[16,8,64,320]{3,2,1,0:T(8,128)(2,1)S(1)} %bitcast.3) | data formatting | bytes 10485760
  183.8 0.0 copy-done.1
  183.8 1.1 copy.29
  (1 shorter events, 0.0 us)
Async XLA Ops:
  0.6 17.5 %copy-start.2 = (bf16[16,8,64,4]{2,3,1,0:T(4,128)(2,1)S(1)}, bf16[16,8,64,4]{2,3,1,0:T(4,128)(2,1)}, u32[]{:S(2)}) copy-start(bf16[16,8,64,4]{2,3,1,0:T(4,128)(2,1)} %param.16) | copy-start | bytes 196612
  1.4 14.1 %collective-permute-start = (bf16[16,1,64,4]{2,3,1,0:T(4,128)(2,1)S(1)}, bf16[16,1,64,4]{2,3,1,0:T(4,128)(2,1)S(1)}, u32[]{:S(2)}, u32[]{:S(2)}) collective-permute-start(bf16[16,1,64,4]{2,3,1,0:T(4,128)(2,1)S(1)} %get-tuple-element.12), channel_id=1, source_target_pairs={{0,1},{1,2},{2,3},{3,4},{4,5},{5,6},{6,7},{8,9},{9,10},{10,11},{11... | collective-permute-start | bytes 24584 | tf_op jit(solution)/shard_map/ppermute | solution.py:393
  6.1 9.5 %collective-permute-start.1 = (bf16[16,1,64,4]{2,3,1,0:T(4,128)(2,1)S(1)}, bf16[16,1,64,4]{2,3,1,0:T(4,128)(2,1)S(1)}, u32[]{:S(2)}, u32[]{:S(2)}) collective-permute-start(bf16[16,1,64,4]{2,3,1,0:T(4,128)(2,1)S(1)} %get-tuple-element.13), channel_id=1, source_target_pairs={{1,0},{2,1},{3,2},{4,3},{5,4},{6,5},{7,6},{9,8},{10,9},{11,10},{12... | collective-permute-start | bytes 24584 | tf_op jit(solution)/shard_map/ppermute | solution.py:394
  170.7 7.1 %copy-start = (bf16[16,8,64,320]{3,2,1,0:T(8,128)(2,1)S(1)}, bf16[16,8,64,320]{3,2,1,0:T(8,128)(2,1)}, u32[]{:S(2)}) copy-start(bf16[16,8,64,320]{3,2,1,0:T(8,128)(2,1)} %get-tuple-element.25) | copy-start | bytes 15728644
  170.7 9.9 %slice-start = ((s8[6291456]{0:T(1024)(128)(4,1)}), s8[4194304]{0:T(1024)(128)(4,1)S(1)}, s32[]{:S(2)}) async-start(s8[6291456]{0:T(1024)(128)(4,1)} %bitcast.2), calls=%async_computation | async-start | bytes 8388608
  177.8 3.3 %slice-start.1 = ((s8[6291456]{0:T(1024)(128)(4,1)}), s8[2097152]{0:T(1024)(128)(4,1)S(1)}, s32[]{:S(2)}) async-start(s8[6291456]{0:T(1024)(128)(4,1)} %bitcast.2), calls=%async_computation.1 | async-start | bytes 4194304
  181.1 2.7 %copy-start.1 = (bf16[16,4,32,320]{3,2,1,0:T(8,128)(2,1)S(1)}, bf16[16,4,32,320]{3,2,1,0:T(8,128)(2,1)}, u32[]{:S(2)}) copy-start(bf16[16,4,32,320]{3,2,1,0:T(8,128)(2,1)} %get-tuple-element.27) | copy-start | bytes 3932164
